TPU v7x, 32 devices: a whole 2x2x4 slice. The times are simulated.
32 devices in a mesh: replica: 4 (over y, core), fsdp: 8 (over z, x).
Axes of the slice: x: 2, y: 2, z: 4, core: 2. Of those that a mesh axis runs over, the one named last changes fastest.
Arguments:
- hidden_states: bfloat16 [4, 2048, 4096], P('replica', 'fsdp'), may hold values from -6 to 6
- norm_gain: bfloat16 [4, 4096], P('replica', 'fsdp'), may hold values from 0.5 to 1.5
- key_weight: bfloat16 [4, 4096, 1024], P('replica', 'fsdp'), may hold values from -0.09375 to 0.09375
- value_weight: bfloat16 [4, 4096, 1024], P('replica', 'fsdp'), may hold values from -0.09375 to 0.09375
- deltas: float32 [4, 256, 4096], P('replica', 'fsdp'), may hold values from -6 to 6
- outer_params: float32 [256, 4096], P('fsdp', 'replica'), may hold values from -6 to 6
- momentum: float32 [256, 4096], P('fsdp', 'replica'), may hold values from -3 to 3
- local_params: bfloat16 [4, 256, 4096], P('replica', 'fsdp'), may hold values from -6 to 6
Outputs:
- keys: bfloat16 [4, 2048, 1024], P('replica', 'fsdp')
- values: bfloat16 [4, 2048, 1024], P('replica', 'fsdp')
- momentum_new: float32 [256, 4096], P('fsdp', 'replica')
- outer_new: float32 [256, 4096], P('fsdp', 'replica')
- local_new: bfloat16 [4, 256, 4096], P('replica', 'fsdp')
All inputs are finite; a program needn't handle non-finite values.
Results may differ from a plain program's by a relative error of at most 0.0085.
Values may be sent and summed in bfloat16 or wider, within the bound.
A program may use at most 128 MiB of HBM per device.

v0:
```python
import jax
import jax.numpy as jnp
from jax import lax
from jax.sharding import PartitionSpec as P

HEAD = 128


def rotate_keys(keys_raw, positions, head_size):
    half_width = head_size // 2
    exponent = jnp.arange(half_width, dtype=jnp.float32) * (2.0 / head_size)
    frequency = jnp.power(jnp.float32(500000.0), -exponent)
    angles = positions.astype(jnp.float32)[:, None] * frequency[None, :]
    cosine_table = jnp.cos(angles)[:, None, :]
    sine_table = jnp.sin(angles)[:, None, :]
    shaped = keys_raw.reshape(keys_raw.shape[0], -1, head_size)
    first_half = shaped[:, :, :half_width]
    second_half = shaped[:, :, half_width:]
    turned = jnp.concatenate(
        [
            first_half * cosine_table - second_half * sine_table,
            second_half * cosine_table + first_half * sine_table,
        ],
        axis=2,
    )
    return turned.reshape(keys_raw.shape)


def per_device(
    hidden_states, norm_gain, key_weight, value_weight, deltas, outer_params, momentum, local_params
):
    states = hidden_states[0]
    squares = jnp.square(states.astype(jnp.float32))
    inv_rms = lax.rsqrt(jnp.mean(squares, axis=1, keepdims=True) + 1e-05)
    gain_rows = lax.all_gather(norm_gain[0], "fsdp", axis=0, tiled=True)
    key_rows = lax.all_gather(key_weight[0], "fsdp", axis=0, tiled=True)
    value_rows = lax.all_gather(value_weight[0], "fsdp", axis=0, tiled=True)
    normed = (states.astype(jnp.float32) * inv_rms * gain_rows.astype(jnp.float32)[None, :]).astype(
        jnp.bfloat16
    )
    keys_raw = jnp.dot(normed, key_rows, preferred_element_type=jnp.float32)
    values_raw = jnp.dot(normed, value_rows, preferred_element_type=jnp.float32)
    positions = jnp.arange(states.shape[0], dtype=jnp.int32)
    rotated = rotate_keys(keys_raw, positions, HEAD)
    replicas = lax.axis_size("replica")
    delta_rows = deltas[0]
    avg_whole = lax.psum(delta_rows.astype(jnp.bfloat16), "replica").astype(jnp.float32) / replicas
    outer_whole = lax.all_gather(outer_params, "replica", axis=1, tiled=True)
    momentum_whole = lax.all_gather(momentum, "replica", axis=1, tiled=True)
    momentum_full = 0.9 * momentum_whole + avg_whole
    outer_rows = outer_whole - 0.7 * (avg_whole + 0.9 * momentum_full)
    width_own = outer_params.shape[1]
    offset = lax.axis_index("replica") * width_own
    momentum_new = lax.dynamic_slice_in_dim(momentum_full, offset, width_own, 1)
    outer_new = lax.dynamic_slice_in_dim(outer_rows, offset, width_own, 1)
    local_new = (0.5 * local_params[0].astype(jnp.float32) + 0.5 * outer_rows).astype(jnp.bfloat16)[
        None
    ]
    return (
        rotated.astype(jnp.bfloat16)[None],
        values_raw.astype(jnp.bfloat16)[None],
        momentum_new,
        outer_new,
        local_new,
    )


def solution(mesh):
    in_specs = (
        P("replica", "fsdp", None),
        P("replica", "fsdp"),
        P("replica", "fsdp", None),
        P("replica", "fsdp", None),
        P("replica", "fsdp", None),
        P("fsdp", "replica"),
        P("fsdp", "replica"),
        P("replica", "fsdp", None),
    )
    out_specs = (
        P("replica", "fsdp", None),
        P("replica", "fsdp", None),
        P("fsdp", "replica"),
        P("fsdp", "replica"),
        P("replica", "fsdp", None),
    )
    return jax.shard_map(
        per_device, mesh=mesh, in_specs=in_specs, out_specs=out_specs, check_vma=False
    )
```

profile of v0, /device:TPU:0, one launch (start us, length us, event | category | flops | bytes accessed | tf_op | source)
XLA Modules:
  0.0 278.0 jit_solution(17915847253404958928)
XLA Ops:
  8.0 0.0 all-reduce.2.cloned.1.call-start
  8.1 1.9 convert_bitcast_fusion.1
  10.0 0.0 all-reduce.2.cloned.1.call-update
  10.0 0.0 all-gather.6.cloned.1.call-start
  10.1 0.5 all-gather.6.cloned.1.call-update
  10.6 0.0 all-gather.8.cloned.1.call-start
  10.6 0.5 all-gather.8.cloned.1.call-update
  11.2 28.9 %all-gather = bf16[1,4096]{1,0:T(2,128)(2,1)S(1)} all-gather(bf16[1,512]{1,0:T(2,128)(2,1)} %param.9), channel_id=2, replica_groups=mesh['replica'=4,'fsdp'=8] {'fsdp'}, dimensions={1}, use_global_device_ids=true | all-gather | bytes 9216 | tf_op jit(solution)/shard_map/all_gather | solution.py:35
  40.2 7.8 %all_gather.19 = f32[32,4096]{1,0:T(8,128)S(1)} all-gather(f32[32,1024]{1,0:T(8,128)} %param.13), channel_id=1, replica_groups=mesh['replica'=4,'fsdp'=8] {'replica'}, dimensions={1}, use_global_device_ids=true | all-gather | bytes 655360 | tf_op jit(solution)/shard_map/all_gather | solution.py:48
  47.9 7.5 %all_gather.18 = f32[32,4096]{1,0:T(8,128)S(1)} all-gather(f32[32,1024]{1,0:T(8,128)} %param.14), channel_id=1, replica_groups=mesh['replica'=4,'fsdp'=8] {'replica'}, dimensions={1}, use_global_device_ids=true | all-gather | bytes 655360 | tf_op jit(solution)/shard_map/all_gather | solution.py:49
  55.4 0.5 fusion.4
  55.9 0.6 add_rsqrt_fusion
  56.5 0.3 multiply_cosine_fusion
  56.8 0.0 all-reduce.2.cloned.1.call-done
  56.8 0.0 copy-done.1
  56.8 1.9 fusion.30
  58.7 0.7 constant_dynamic-slice_fusion
  59.4 80.3 %all-gather.6.cloned.1.call-done = bf16[1,4096,1024]{2,1,0:T(8,128)(2,1)} async-done(((bf16[1,512,1024]{2,1,0:T(8,128)(2,1)}), bf16[1,4096,1024]{2,1,0:T(8,128)(2,1)}) %all-gather.6.cloned.1.call-update) | async-done | bytes 8388624 | tf_op jit(solution)/shard_map/all_gather | solution.py:36
  139.7 11.4 %copy.13 = bf16[1024,4096]{1,0:T(8,128)(2,1)} copy(bf16[1024,4096]{0,1:T(8,128)(2,1)} %bitcast.44) | data formatting | bytes 16777216 | tf_op jit(solution)/shard_map/dot_general | solution.py:41
  151.1 5.8 %fusion.10 = f32[256,8,128]{0,2,1:T(8,128)S(1)} fusion(bf16[8,128,4096]{2,1,0:T(8,128)(2,1)} %bitcast.45, bf16[1,256,4096]{2,1,0:T(8,128)(2,1)S(1)} %copy-done, f32[4096]{0:T(1024)S(1)} %bitcast.47, f32[256]{0:T(256)S(1)} %copy-done.2), kind=kOutput, calls=%fused_computation.12 | convolution fusion | flops 2151677952 | bytes 11551744 | tf_op jit(solution)/shard_map/dot_general | solution.py:41
  156.9 0.1 subtract_convert_fusion
  157.1 1.0 copy.14
  158.1 105.9 %all-gather.8.cloned.1.call-done = bf16[1,4096,1024]{2,1,0:T(8,128)(2,1)} async-done(((bf16[1,512,1024]{2,1,0:T(8,128)(2,1)}), bf16[1,4096,1024]{2,1,0:T(8,128)(2,1)}) %all-gather.8.cloned.1.call-update) | async-done | bytes 8388624 | tf_op jit(solution)/shard_map/all_gather | solution.py:37
  264.0 6.6 %fusion.22 = bf16[1,256,1024]{2,1,0:T(8,128)(2,1)} fusion(bf16[1,4096,1024]{2,1,0:T(8,128)(2,1)} %all-gather.8.cloned.1.call-done, bf16[1,256,4096]{2,1,0:T(8,128)(2,1)S(1)} %copy-done, f32[4096]{0:T(1024)S(1)} %bitcast.48, f32[256]{0:T(256)S(1)} %copy-done.2), kind=kOutput, calls=%fused_computation.18 | convolution fusion | flops 2151940096 | bytes 11027456 | tf_op jit(solution)/shard_map/dot_general | solution.py:42
  (9 shorter events, 0.1 us)
Async XLA Ops:
  8.0 47.4 %copy-start = (bf16[1,256,4096]{2,1,0:T(8,128)(2,1)S(1)}, bf16[1,256,4096]{2,1,0:T(8,128)(2,1)}, u32[]{:S(2)}) copy-start(bf16[1,256,4096]{2,1,0:T(8,128)(2,1)} %param.8) | copy-start | bytes 6291460
  8.0 48.8 %copy-start.1 = (bf16[1,32,4096]{2,1,0:T(8,128)(2,1)S(1)}, bf16[1,32,4096]{2,1,0:T(8,128)(2,1)}, u32[]{:S(2)}) copy-start(bf16[1,32,4096]{2,1,0:T(8,128)(2,1)} %param.15) | copy-start | bytes 786436
  8.0 48.8 %all-reduce.2.cloned.1.call-start = ((), (), s32[]{:S(2)}) async-start(), calls=%async_computation | async-start | bytes 524288 | tf_op jit(solution)/shard_map/psum | solution.py:47
  10.0 129.7 %all-gather.6.cloned.1.call-start = ((), (), s32[]{:S(2)}) async-start(), calls=%async_computation.1 | async-start | bytes 9437184 | tf_op jit(solution)/shard_map/all_gather | solution.py:36
  10.6 253.4 %all-gather.8.cloned.1.call-start = ((), (), s32[]{:S(2)}) async-start(), calls=%async_computation.2 | async-start | bytes 9437184 | tf_op jit(solution)/shard_map/all_gather | solution.py:37
  139.7 11.4 %copy-start.2 = (f32[256]{0:T(256)S(1)}, f32[256]{0:T(256)}, u32[]{:S(2)}) copy-start(f32[256]{0:T(256)} %add_rsqrt_fusion) | copy-start | bytes 3076
Sparse Core Ops, SparseCore 0:
  11.7 35.1 all-reduce.1
Sparse Core Ops, SparseCore 1:
  12.6 127.0 all-gather.5
  141.7 122.3 all-gather.7
where the time goes:
time: 279 us; the launch traced here: 278 us
  waiting for transfers between devices  187 us (67%)
  blocking collectives  44.2 us (16%)
  between operations  15.6 us (6%)
  local copies, waits for them, and re-layouts  13.2 us (5%)
  matrix products  12.4 us (4%)
  other arithmetic  5.36 us (2%)
    all_gather x1, waiting for transfers between devices, per_device(): value_rows = lax.all_gather(value_weight[0], 'fsdp', axis=0, tiled=True)  106 us
    all_gather x1, waiting for transfers between devices, per_device(): key_rows = lax.all_gather(key_weight[0], 'fsdp', axis=0, tiled=True)  80.3 us
    all_gather x1, blocking collectives, per_device(): gain_rows = lax.all_gather(norm_gain[0], 'fsdp', axis=0, tiled=True)  28.9 us
    dot_general x1, local copies, waits for them, and re-layouts, per_device(): keys_raw = jnp.dot(normed, key_rows, preferred_element_type=jnp.float32)  11.4 us
    all_gather x1, blocking collectives, per_device(): outer_whole = lax.all_gather(outer_params, 'replica', axis=1, tiled=True)  7.78 us
    all_gather x1, blocking collectives, per_device(): momentum_whole = lax.all_gather(momentum, 'replica', axis=1, tiled=True)  7.48 us
    dot_general x1, matrix products, per_device(): values_raw = jnp.dot(normed, value_rows, preferred_element_type=jnp.float32)  6.55 us
    dot_general x1, matrix products, per_device(): keys_raw = jnp.dot(normed, key_rows, preferred_element_type=jnp.float32)  5.82 us
  transfers between devices with their start and end apart: 3, of which 2 were waited for; matrix products, arithmetic and copies ran while one was open for 8% of the time, Pallas kernels for 0%

commit v1 on v0

v1 whole, which is shorter than its diff:
```python
import functools

import jax
import jax.numpy as jnp
from jax import lax
from jax.experimental import pallas as pl
from jax.experimental.pallas import tpu as pltpu
from jax.sharding import PartitionSpec as P

HEAD = 128
MESH = pl.DeviceIdType.MESH


def rotation_tables(tokens, head_size):
    half_width = head_size // 2
    exponent = jnp.arange(half_width, dtype=jnp.float32) * (2.0 / head_size)
    frequency = jnp.power(jnp.float32(500000.0), -exponent)
    angles = jnp.arange(tokens, dtype=jnp.int32).astype(jnp.float32)[:, None] * frequency[None, :]
    cosine, sine = jnp.cos(angles), jnp.sin(angles)
    return jnp.concatenate([cosine, cosine], axis=1), jnp.concatenate([-sine, sine], axis=1)


def stage_plan(groups):
    plan, left, bit = [], list(range(groups)), 1
    while bit < groups:
        plan.append((bit, [b for b in left if b & bit], [b for b in left if not b & bit]))
        left = plan[-1][2]
        bit *= 2
    return plan


def kernel(
    groups, replicas, width,
    hs, gain, kw, vw, cosine, sine, deltas, outer, momentum, local,
    keys, values, momentum_new, outer_new, local_new,
    hs_v, gains, a_in, a_scaled, weights, inv, partial, d_in, o_in, *rest,
):
    plan = stage_plan(groups)
    stages = len(plan)
    c_out, c_in, rest = rest[:stages], rest[stages : 2 * stages], rest[2 * stages :]
    hs_sem, g_sem, a_sem, b_sem, own_sem, c_sem, d_sem, o_sem = rest

    r, f = lax.axis_index("replica"), lax.axis_index("fsdp")
    x, z = lax.rem(f, 2), lax.div(f, 2)
    tokens, depth = hs.shape[0], kw.shape[0]
    quarter = 2 * depth
    per_weight = kw.shape[1] // width
    chunks = 2 * per_weight
    own_w = outer.shape[1]

    def group_at(offset):
        g, bit = z, 1
        while bit < groups:
            if offset & bit:
                g = g + bit * (1 - 2 * lax.rem(lax.div(g, bit), 2))
            bit *= 2
        return g

    def peer(offset):
        return {"fsdp": 2 * group_at(offset) + x}

    partner = {"fsdp": f + 1 - 2 * x}

    def replica_at(j):
        return lax.rem(r + j, replicas)

    barrier = pltpu.get_barrier_semaphore()
    pl.semaphore_signal(barrier, inc=1, device_id=partner, device_id_type=MESH)
    for b in range(1, groups):
        pl.semaphore_signal(barrier, inc=1, device_id=peer(b), device_id_type=MESH)
    for j in range(1, replicas):
        pl.semaphore_signal(
            barrier, inc=1, device_id={"replica": replica_at(j)}, device_id_type=MESH
        )

    def remote(src, dst, sems, index, target):
        return pltpu.make_async_remote_copy(
            src_ref=src, dst_ref=dst, send_sem=sems.at[(0,) + index],
            recv_sem=sems.at[(1,) + index], device_id=target, device_id_type=MESH,
        )

    hs_copy = pltpu.make_async_copy(hs, hs_v, hs_sem)
    hs_copy.start()
    rows = pl.ds(pl.multiple_of(x * depth, depth), depth)
    own_copies = []
    for c in range(chunks):
        source = (kw if c < per_weight else vw).at[:, pl.ds((c % per_weight) * width, width)]
        own_copies.append(pltpu.make_async_copy(source, weights.at[c, rows], own_sem.at[c]))
        own_copies[-1].start()

    pl.semaphore_wait(barrier, groups + replicas - 1)

    gain_copy = remote(gain, gains.at[x], g_sem, (), partner)
    gain_copy.start()
    a_copies = {}
    order = plan[0][1] + [b for b in plan[0][2] if b]
    for b in order:
        columns = pl.ds(pl.multiple_of(group_at(b) * quarter, quarter), quarter)
        a_copies[b] = remote(hs.at[:, columns], a_in.at[b - 1], a_sem, (b - 1,), peer(b))
        a_copies[b].start()
    b_copies = []
    for c in range(chunks):
        source = (kw if c < per_weight else vw).at[:, pl.ds((c % per_weight) * width, width)]
        b_copies.append(remote(source, weights.at[c, rows], b_sem, (c,), partner))
        b_copies[-1].start()
    d_copies = []
    for j in range(1, replicas):
        columns = pl.ds(pl.multiple_of(replica_at(j) * own_w, own_w), own_w)
        d_copies.append(
            remote(
                deltas.at[:, columns], d_in.at[j - 1], d_sem, (j - 1,), {"replica": replica_at(j)}
            )
        )
        d_copies[-1].start()

    def c_copy(stage, c):
        return remote(
            c_out[stage].at[c], c_in[stage].at[c], c_sem, (stage, c), peer(plan[stage][0])
        )

    def b_wait(c):
        pltpu.make_async_copy(
            kw.at[:, pl.ds(0, width)], weights.at[c, rows], own_sem.at[c]
        ).wait()
        remote(
            kw.at[:, pl.ds(0, width)], weights.at[c, rows], b_sem, (c,), partner
        ).wait_recv()

    hs_copy.wait()
    total = jnp.zeros((tokens, 1), jnp.float32)
    features = hs.shape[1]
    for k in range(groups):
        part = hs_v[:, k * quarter : (k + 1) * quarter].astype(jnp.float32)
        total += jnp.sum(part * part, axis=1, keepdims=True)
    inv[...] = jnp.broadcast_to(lax.rsqrt(total / features + 1e-05), inv.shape)

    gains[x] = gain[...]
    gain_copy.wait()
    gain_row = jnp.concatenate([gains[0], gains[1]], axis=1)

    def scale(b, block):
        a_scaled[b] = (block.astype(jnp.float32) * gain_row).astype(jnp.bfloat16)

    scale(0, hs_v[:, pl.ds(pl.multiple_of(z * quarter, quarter), quarter)])
    for b in plan[0][1]:
        a_copies[b].wait_recv()
        scale(b, a_in[b - 1])

    def product(b, c):
        return jnp.dot(a_scaled[b], weights[c], preferred_element_type=jnp.float32)

    @pl.loop(0, chunks)
    def _(c):
        b_wait(c)
        for i, b in enumerate(plan[0][1]):
            c_out[0][c, i] = product(b, c).astype(jnp.bfloat16)
        c_copy(0, c).start()

    avg = deltas[:, pl.ds(pl.multiple_of(r * own_w, own_w), own_w)]
    for j in range(1, replicas):
        d_copies[j - 1].wait_recv()
        avg += d_in[j - 1]
    avg = avg / replicas
    moved = 0.9 * momentum[...] + avg
    momentum_new[...] = moved
    outer_new[...] = outer[...] - 0.7 * (avg + 0.9 * moved)

    for b in plan[0][2]:
        if b:
            a_copies[b].wait_recv()
            scale(b, a_in[b - 1])

    o_copies = []
    for j in range(1, replicas):
        o_copies.append(
            remote(outer_new, o_in.at[j - 1], o_sem, (j - 1,), {"replica": replica_at(j)})
        )
        o_copies[-1].start()

    for stage in range(stages):
        bit, sent, kept = plan[stage]
        last = stage == stages - 1
        upcoming = [] if last else plan[stage + 1][1]

        def summed(b, c):
            before = product(b, c) if stage == 0 else partial[b, c]
            return before + c_in[stage][c, sent.index(b + bit)].astype(jnp.float32)

        if not last:

            @pl.loop(0, chunks)
            def _(c):
                c_copy(stage, c).wait_recv()
                for b in kept:
                    value = summed(b, c)
                    if b in upcoming:
                        c_out[stage + 1][c, upcoming.index(b)] = value.astype(jnp.bfloat16)
                    else:
                        partial[b, c] = value
                c_copy(stage + 1, c).start()

        if stage == 0:
            half = jnp.float32(0.5)
            mine = pl.ds(pl.multiple_of(r * own_w, own_w), own_w)
            local_new[:, mine] = (
                half * local[:, mine].astype(jnp.float32) + half * outer_new[...]
            ).astype(jnp.bfloat16)
            for j in range(1, replicas):
                o_copies[j - 1].wait_recv()
                theirs = pl.ds(
                    pl.multiple_of(lax.rem(r + replicas - j, replicas) * own_w, own_w), own_w
                )
                local_new[:, theirs] = (
                    half * local[:, theirs].astype(jnp.float32) + half * o_in[j - 1]
                ).astype(jnp.bfloat16)

        if last:

            @pl.loop(0, per_weight)
            def _(c):
                c_copy(stage, c).wait_recv()
                value = summed(0, c) * inv[:, 0:1]
                for h in range(width // HEAD):
                    head = value[:, h * HEAD : (h + 1) * HEAD]
                    turned = head * cosine[...] + pltpu.roll(head, HEAD // 2, 1) * sine[...]
                    at = pl.ds(pl.multiple_of(c * width + h * HEAD, HEAD), HEAD)
                    keys[:, at] = turned.astype(jnp.bfloat16)

            @pl.loop(0, per_weight)
            def _(c):
                c_copy(stage, c + per_weight).wait_recv()
                value = summed(0, c + per_weight) * inv[:, 0:1]
                at = pl.ds(pl.multiple_of(c * width, width), width)
                values[:, at] = value.astype(jnp.bfloat16)

    for copy in list(a_copies.values()) + b_copies + d_copies + o_copies:
        copy.wait_send()
    for stage in range(stages):

        @pl.loop(0, chunks)
        def _(c):
            c_copy(stage, c).wait_send()


def per_device(
    groups, replicas,
    hidden_states, norm_gain, key_weight, value_weight, deltas, outer_params, momentum, local_params,
):
    hs, kw, vw = hidden_states[0], key_weight[0], value_weight[0]
    tokens, features = hs.shape
    depth, kv = kw.shape
    width = 2 * HEAD
    chunks = 2 * kv // width
    cosine, sine = rotation_tables(tokens, HEAD)
    plan = stage_plan(groups)
    blocks = [pltpu.VMEM((chunks, len(p[1]), tokens, width), jnp.bfloat16) for p in plan]
    own = outer_params.shape
    vmem = pl.BlockSpec(memory_space=pltpu.VMEM)
    hbm = pl.BlockSpec(memory_space=pl.ANY)
    dma = pltpu.SemaphoreType.DMA
    keys, values, momentum_new, outer_new, local_new = pl.pallas_call(
        functools.partial(kernel, groups, replicas, width),
        out_shape=(
            jax.ShapeDtypeStruct((tokens, kv), jnp.bfloat16),
            jax.ShapeDtypeStruct((tokens, kv), jnp.bfloat16),
            jax.ShapeDtypeStruct(own, jnp.float32),
            jax.ShapeDtypeStruct(own, jnp.float32),
            jax.ShapeDtypeStruct(local_params.shape[1:], jnp.bfloat16),
        ),
        in_specs=[hbm, vmem, hbm, hbm] + [vmem] * 6,
        out_specs=[vmem] * 5,
        scratch_shapes=[
            pltpu.VMEM((tokens, features), jnp.bfloat16),
            pltpu.VMEM((2, 1, depth), jnp.float32),
            pltpu.VMEM((groups - 1, tokens, 2 * depth), jnp.bfloat16),
            pltpu.VMEM((groups, tokens, 2 * depth), jnp.bfloat16),
            pltpu.VMEM((chunks, 2 * depth, width), jnp.bfloat16),
            pltpu.VMEM((tokens, HEAD), jnp.float32),
            pltpu.VMEM((max(p + 1 for p in plan[0][2] if not p & 2), chunks, tokens, width), jnp.float32),
            pltpu.VMEM((replicas - 1,) + own, jnp.float32),
            pltpu.VMEM((replicas - 1,) + own, jnp.float32),
            *blocks,
            *blocks,
            dma,
            dma((2,)),
            dma((2, groups - 1)),
            dma((2, chunks)),
            dma((chunks,)),
            dma((2, len(plan), chunks)),
            dma((2, replicas - 1)),
            dma((2, replicas - 1)),
        ],
        compiler_params=pltpu.CompilerParams(
            collective_id=0, has_side_effects=True, vmem_limit_bytes=60 * 1024 * 1024
        ),
    )(
        hs, norm_gain.astype(jnp.float32), kw, vw, cosine, sine,
        deltas[0], outer_params, momentum, local_params[0],
    )
    return keys[None], values[None], momentum_new, outer_new, local_new[None]


def solution(mesh):
    in_specs = (
        P("replica", "fsdp", None),
        P("replica", "fsdp"),
        P("replica", "fsdp", None),
        P("replica", "fsdp", None),
        P("replica", "fsdp", None),
        P("fsdp", "replica"),
        P("fsdp", "replica"),
        P("replica", "fsdp", None),
    )
    out_specs = (
        P("replica", "fsdp", None),
        P("replica", "fsdp", None),
        P("fsdp", "replica"),
        P("fsdp", "replica"),
        P("replica", "fsdp", None),
    )
    groups, replicas = mesh.shape["fsdp"] // 2, mesh.shape["replica"]
    return jax.shard_map(
        functools.partial(per_device, groups, replicas),
        mesh=mesh, in_specs=in_specs, out_specs=out_specs, check_vma=False,
    )
```

time: 279 us -> 125 us (0.45)
  waiting for transfers between devices: 187 us -> 0 us
  Pallas kernels: 0 us -> 115 us
  blocking collectives: 44.2 us -> 0 us
  between operations: 15.6 us -> 0.68 us
  matrix products: 12.4 us -> 0 us
  local copies, waits for them, and re-layouts: 13.2 us -> 5.82 us
    all_gather x2 -> x0, waiting for transfers between devices: 186 us -> none  [the longest x1 106 us: per_device(): value_rows = lax.all_gather(value_weight[0], 'fsdp', axis=0, tiled=True)]
    pallas_call x0 -> x1, Pallas kernels: none -> 115 us  [per_device(): pl.pallas_call(functools.partial(kernel, groups, replicas, width), out_sh...]
    all_gather x3 -> x0, blocking collectives: 44.2 us -> none  [the longest x1 28.9 us: per_device(): gain_rows = lax.all_gather(norm_gain[0], 'fsdp', axis=0, tiled=True)]
    dot_general x2 -> x0, matrix products: 12.4 us -> none  [the longest x1 6.55 us: per_device(): values_raw = jnp.dot(normed, value_rows, preferred_element_type=jnp.float32)]
    dot_general x1 -> x0, local copies, waits for them, and re-layouts: 11.4 us -> none  [per_device(): keys_raw = jnp.dot(normed, key_rows, preferred_element_type=jnp.float32)]
    unnamed x7 -> x11, local copies, waits for them, and re-layouts: 1.01 us -> 5.82 us
  transfers between devices with their start and end apart: 3 -> 0, of which waited for: 2 -> 0; matrix products, arithmetic and copies ran while one was open for 8% -> 0% of each run, Pallas kernels for 0% -> 0%
where the time goes in v1:
time: 125 us; the launch traced here: 124 us
  Pallas kernels  115 us (92%)
  local copies, waits for them, and re-layouts  5.82 us (5%)
  other arithmetic  2.65 us (2%)
    pallas_call x1, Pallas kernels, per_device(): pl.pallas_call(functools.partial(kernel, groups, replicas, width), out_sh...  115 us
    unnamed x11, local copies, waits for them, and re-layouts  5.82 us

profile of v1, /device:TPU:0, one launch (start us, length us, event | category | flops | bytes accessed | tf_op | source)
XLA Modules:
  0.0 124.3 jit_solution(17376530506199069494)
XLA Ops:
  0.7 1.3 %convert_element_type.16.gain = f32[1,512]{1,0:T(1,128)} convert(bf16[1,512]{1,0:T(2,128)(2,1)} %param.9) | non-fusion elementwise | flops 512 | bytes 3072 | tf_op jit(solution)/shard_map/convert_element_type | solution.py:297
  1.9 0.5 fusion
  2.5 0.8 pad_maximum_fusion
  3.3 115.2 %shard_map.119 = (bf16[256,1024]{1,0:T(8,128)(2,1)}, bf16[256,1024]{1,0:T(8,128)(2,1)}, f32[32,1024]{1,0:T(8,128)}, f32[32,1024]{1,0:T(8,128)}, bf16[32,4096]{1,0:T(8,128)(2,1)}) custom-call(bf16[256,4096]{1,0:T(8,128)(2,1)} %bitcast.8, f32[1,512]{1,0:T(1,128)} %convert_element_type.16.gain, bf16[512,1024]{1,0:T(8,128)(2,1)} %bitcast.9, ...), custom_call_target="tpu_custom_call" | custom-call | tf_op jit(solution)/shard_map/pallas_call | solution.py:261
  118.5 0.0 copy-start.2
  118.5 0.0 copy-start.1
  118.5 0.0 copy-start
  118.5 1.9 %copy.18 = bf16[1,256,1024]{2,1,0:T(8,128)(2,1)} copy(bf16[1,256,1024]{2,1,0:T(8,128)(2,1)} %bitcast.13) | data formatting | bytes 1048576
  120.5 1.9 %copy.19 = bf16[1,256,1024]{2,1,0:T(8,128)(2,1)} copy(bf16[1,256,1024]{2,1,0:T(8,128)(2,1)} %bitcast.12) | data formatting | bytes 1048576
  122.3 0.0 copy-done.2
  122.3 0.7 copy.20
  123.0 0.0 copy-done.1
  123.0 0.7 copy.21
  123.6 0.0 copy-done
  123.6 0.7 copy.22
  (2 shorter events, 0.0 us)
Async XLA Ops:
  118.5 3.8 %copy-start.2 = (f32[32,1024]{1,0:T(8,128)S(1)}, f32[32,1024]{1,0:T(8,128)}, u32[]{:S(2)}) copy-start(f32[32,1024]{1,0:T(8,128)} %get-tuple-element.27) | copy-start | bytes 393220
  118.5 4.5 %copy-start.1 = (f32[32,1024]{1,0:T(8,128)S(1)}, f32[32,1024]{1,0:T(8,128)}, u32[]{:S(2)}) copy-start(f32[32,1024]{1,0:T(8,128)} %get-tuple-element.28) | copy-start | bytes 393220
  118.5 5.1 %copy-start = (bf16[32,4096]{1,0:T(8,128)(2,1)S(1)}, bf16[32,4096]{1,0:T(8,128)(2,1)}, u32[]{:S(2)}) copy-start(bf16[32,4096]{1,0:T(8,128)(2,1)} %get-tuple-element.14) | copy-start | bytes 786436

commit v2 on v1

--- a/solution.py
+++ b/solution.py
@@ -2,6 +2,7 @@
 
 import jax
 import jax.numpy as jnp
+import numpy as np
 from jax import lax
 from jax.experimental import pallas as pl
 from jax.experimental.pallas import tpu as pltpu
@@ -13,11 +14,26 @@
 
 def rotation_tables(tokens, head_size):
     half_width = head_size // 2
-    exponent = jnp.arange(half_width, dtype=jnp.float32) * (2.0 / head_size)
-    frequency = jnp.power(jnp.float32(500000.0), -exponent)
-    angles = jnp.arange(tokens, dtype=jnp.int32).astype(jnp.float32)[:, None] * frequency[None, :]
-    cosine, sine = jnp.cos(angles), jnp.sin(angles)
-    return jnp.concatenate([cosine, cosine], axis=1), jnp.concatenate([-sine, sine], axis=1)
+    exponent = np.arange(half_width, dtype=np.float32) * np.float32(2.0 / head_size)
+    frequency = np.power(np.float32(500000.0), -exponent)
+    angles = np.arange(tokens, dtype=np.float32)[:, None] * frequency[None, :]
+    cosine, sine = np.cos(angles), np.sin(angles)
+    return (
+        jnp.asarray(np.concatenate([cosine, cosine], axis=1)),
+        jnp.asarray(np.concatenate([-sine, sine], axis=1)),
+    )
+
+
+def write_out(*refs):
+    count = len(refs) // 2
+    sems = refs[-1]
+    copies = [
+        pltpu.make_async_copy(refs[i], refs[count + i], sems.at[i]) for i in range(count)
+    ]
+    for copy in copies:
+        copy.start()
+    for copy in copies:
+        copy.wait()
 
 
 def stage_plan(groups):
@@ -93,11 +109,14 @@
     gain_copy = remote(gain, gains.at[x], g_sem, (), partner)
     gain_copy.start()
     a_copies = {}
-    order = plan[0][1] + [b for b in plan[0][2] if b]
-    for b in order:
-        columns = pl.ds(pl.multiple_of(group_at(b) * quarter, quarter), quarter)
-        a_copies[b] = remote(hs.at[:, columns], a_in.at[b - 1], a_sem, (b - 1,), peer(b))
-        a_copies[b].start()
+
+    def send_tokens(offsets):
+        for b in offsets:
+            columns = pl.ds(pl.multiple_of(group_at(b) * quarter, quarter), quarter)
+            a_copies[b] = remote(hs.at[:, columns], a_in.at[b - 1], a_sem, (b - 1,), peer(b))
+            a_copies[b].start()
+
+    send_tokens(plan[0][1])
     b_copies = []
     for c in range(chunks):
         source = (kw if c < per_weight else vw).at[:, pl.ds((c % per_weight) * width, width)]
@@ -136,7 +155,7 @@
 
     gains[x] = gain[...]
     gain_copy.wait()
-    gain_row = jnp.concatenate([gains[0], gains[1]], axis=1)
+    gain_row = jnp.concatenate([gains[0], gains[1]], axis=1).astype(jnp.float32)
 
     def scale(b, block):
         a_scaled[b] = (block.astype(jnp.float32) * gain_row).astype(jnp.bfloat16)
@@ -149,12 +168,15 @@
     def product(b, c):
         return jnp.dot(a_scaled[b], weights[c], preferred_element_type=jnp.float32)
 
-    @pl.loop(0, chunks)
-    def _(c):
+    def first_products(c):
         b_wait(c)
         for i, b in enumerate(plan[0][1]):
             c_out[0][c, i] = product(b, c).astype(jnp.bfloat16)
         c_copy(0, c).start()
+
+    pl.loop(0, 1)(first_products)
+    send_tokens([b for b in plan[0][2] if b])
+    pl.loop(1, chunks)(first_products)
 
     avg = deltas[:, pl.ds(pl.multiple_of(r * own_w, own_w), own_w)]
     for j in range(1, replicas):
@@ -258,7 +280,7 @@
     vmem = pl.BlockSpec(memory_space=pltpu.VMEM)
     hbm = pl.BlockSpec(memory_space=pl.ANY)
     dma = pltpu.SemaphoreType.DMA
-    keys, values, momentum_new, outer_new, local_new = pl.pallas_call(
+    results = pl.pallas_call(
         functools.partial(kernel, groups, replicas, width),
         out_shape=(
             jax.ShapeDtypeStruct((tokens, kv), jnp.bfloat16),
@@ -271,7 +293,7 @@
         out_specs=[vmem] * 5,
         scratch_shapes=[
             pltpu.VMEM((tokens, features), jnp.bfloat16),
-            pltpu.VMEM((2, 1, depth), jnp.float32),
+            pltpu.VMEM((2, 1, depth), jnp.bfloat16),
             pltpu.VMEM((groups - 1, tokens, 2 * depth), jnp.bfloat16),
             pltpu.VMEM((groups, tokens, 2 * depth), jnp.bfloat16),
             pltpu.VMEM((chunks, 2 * depth, width), jnp.bfloat16),
@@ -294,9 +316,17 @@
             collective_id=0, has_side_effects=True, vmem_limit_bytes=60 * 1024 * 1024
         ),
     )(
-        hs, norm_gain.astype(jnp.float32), kw, vw, cosine, sine,
+        hs, norm_gain, kw, vw, cosine, sine,
         deltas[0], outer_params, momentum, local_params[0],
     )
+    keys, values, momentum_new, outer_new, local_new = pl.pallas_call(
+        write_out,
+        out_shape=tuple(jax.ShapeDtypeStruct(a.shape, a.dtype) for a in results),
+        in_specs=[hbm] * 5,
+        out_specs=[hbm] * 5,
+        scratch_shapes=[dma((5,))],
+        compiler_params=pltpu.CompilerParams(vmem_limit_bytes=1024 * 1024),
+    )(*results)
     return keys[None], values[None], momentum_new, outer_new, local_new[None]
 
 

time: 125 us -> 124 us (level)
  Pallas kernels: 115 us -> 118 us
  other arithmetic: 2.65 us -> 0 us
    pallas_call x1, Pallas kernels: 115 us -> 117 us  [per_device(): pl.pallas_call(functools.partial(kernel, groups, replicas, width), out_sh...]
    convert_element_type x2 -> x0, other arithmetic: 1.27 us -> none  [the longest x1 1.26 us: per_device(): norm_gain.astype(jnp.float32)]
    unnamed x11 -> x10, local copies, waits for them, and re-layouts: 5.82 us -> 4.83 us
where the time goes in v2:
time: 124 us
  Pallas kernels  118 us (95%)
  local copies, waits for them, and re-layouts  4.83 us (4%)
    pallas_call x1, Pallas kernels, per_device(): pl.pallas_call(functools.partial(kernel, groups, replicas, width), out_sh...  117 us
    unnamed x10, local copies, waits for them, and re-layouts  4.83 us

profile of v2, /device:TPU:0, one launch (start us, length us, event | category | flops | bytes accessed | tf_op | source)
XLA Modules:
  0.0 123.9 jit_solution(15117643022937232996)
XLA Ops:
  0.6 117.2 %shard_map.137 = (bf16[256,1024]{1,0:T(8,128)(2,1)}, bf16[256,1024]{1,0:T(8,128)(2,1)}, f32[32,1024]{1,0:T(8,128)}, f32[32,1024]{1,0:T(8,128)}, bf16[32,4096]{1,0:T(8,128)(2,1)}) custom-call(bf16[256,4096]{1,0:T(8,128)(2,1)} %bitcast.8, bf16[1,512]{1,0:T(2,128)(2,1)} %gain.1, bf16[512,1024]{1,0:T(8,128)(2,1)} %bitcast.9, bf16[512,1024]{1,0:T(8,128)(2,1)} %bitcast.10, ...), custom_call_target="tpu_custom_call" | custom-call | tf_op jit(solution)/shard_map/pallas_call | solution.py:283
  117.9 0.0 copy-start
  117.9 1.0 copy-done
  118.9 0.0 copy-start.1
  118.9 1.0 copy-done.1
  119.9 0.0 copy-start.2
  119.9 0.9 copy-done.2
  120.9 0.0 copy-start.3
  120.9 0.9 copy-done.3
  121.8 0.0 copy-start.4
  121.8 0.9 copy-done.4
  122.7 1.2 shard_map.138
Async XLA Ops:
  117.9 1.0 copy-start
  118.9 1.0 copy-start.1
  119.9 0.9 copy-start.2
  120.9 0.9 copy-start.3
  121.8 0.9 copy-start.4

commit v3 on v2

--- a/solution.py
+++ b/solution.py
@@ -47,14 +47,16 @@
 
 def kernel(
     groups, replicas, width,
-    hs, gain, kw, vw, cosine, sine, deltas, outer, momentum, local,
+    hs, gain, kw, vw, cosine_in, sine_in, deltas, outer_in, momentum_in, local_in,
+    keys_out, values_out, momentum_out, outer_out, local_out,
+    cosine, sine, deltas_own, outer, momentum, local,
     keys, values, momentum_new, outer_new, local_new,
     hs_v, gains, a_in, a_scaled, weights, inv, partial, d_in, o_in, *rest,
 ):
     plan = stage_plan(groups)
     stages = len(plan)
     c_out, c_in, rest = rest[:stages], rest[stages : 2 * stages], rest[2 * stages :]
-    hs_sem, g_sem, a_sem, b_sem, own_sem, c_sem, d_sem, o_sem = rest
+    hs_sem, g_sem, a_sem, b_sem, own_sem, c_sem, d_sem, o_sem, load_sem, store_sem = rest
 
     r, f = lax.axis_index("replica"), lax.axis_index("fsdp")
     x, z = lax.rem(f, 2), lax.div(f, 2)
@@ -95,8 +97,22 @@
             recv_sem=sems.at[(1,) + index], device_id=target, device_id_type=MESH,
         )
 
+    mine = pl.ds(pl.multiple_of(r * own_w, own_w), own_w)
     hs_copy = pltpu.make_async_copy(hs, hs_v, hs_sem)
     hs_copy.start()
+    loads = [
+        pltpu.make_async_copy(source, target, load_sem.at[i])
+        for i, (source, target) in enumerate(
+            (
+                (deltas.at[:, mine], deltas_own),
+                (outer_in, outer),
+                (momentum_in, momentum),
+                (local_in, local),
+                (cosine_in, cosine),
+                (sine_in, sine),
+            )
+        )
+    ]
     rows = pl.ds(pl.multiple_of(x * depth, depth), depth)
     own_copies = []
     for c in range(chunks):
@@ -132,6 +148,18 @@
         )
         d_copies[-1].start()
 
+    for copy in loads:
+        copy.start()
+
+    def store(i, source, target):
+        copy = pltpu.make_async_copy(source, target, store_sem.at[i])
+        copy.start()
+        return copy
+
+    def result_copy(source, target, c, sem):
+        at = pl.ds(pl.multiple_of(c * width, width), width)
+        return pltpu.make_async_copy(source.at[:, at], target.at[:, at], store_sem.at[sem])
+
     def c_copy(stage, c):
         return remote(
             c_out[stage].at[c], c_in[stage].at[c], c_sem, (stage, c), peer(plan[stage][0])
@@ -178,7 +206,9 @@
     send_tokens([b for b in plan[0][2] if b])
     pl.loop(1, chunks)(first_products)
 
-    avg = deltas[:, pl.ds(pl.multiple_of(r * own_w, own_w), own_w)]
+    for copy in loads:
+        copy.wait()
+    avg = deltas_own[...]
     for j in range(1, replicas):
         d_copies[j - 1].wait_recv()
         avg += d_in[j - 1]
@@ -186,6 +216,7 @@
     moved = 0.9 * momentum[...] + avg
     momentum_new[...] = moved
     outer_new[...] = outer[...] - 0.7 * (avg + 0.9 * moved)
+    stores = [store(0, momentum_new, momentum_out), store(1, outer_new, outer_out)]
 
     for b in plan[0][2]:
         if b:
@@ -223,7 +254,6 @@
 
         if stage == 0:
             half = jnp.float32(0.5)
-            mine = pl.ds(pl.multiple_of(r * own_w, own_w), own_w)
             local_new[:, mine] = (
                 half * local[:, mine].astype(jnp.float32) + half * outer_new[...]
             ).astype(jnp.bfloat16)
@@ -235,6 +265,7 @@
                 local_new[:, theirs] = (
                     half * local[:, theirs].astype(jnp.float32) + half * o_in[j - 1]
                 ).astype(jnp.bfloat16)
+            stores.append(store(2, local_new, local_out))
 
         if last:
 
@@ -247,6 +278,7 @@
                     turned = head * cosine[...] + pltpu.roll(head, HEAD // 2, 1) * sine[...]
                     at = pl.ds(pl.multiple_of(c * width + h * HEAD, HEAD), HEAD)
                     keys[:, at] = turned.astype(jnp.bfloat16)
+                result_copy(keys, keys_out, c, 3 + c).start()
 
             @pl.loop(0, per_weight)
             def _(c):
@@ -254,6 +286,15 @@
                 value = summed(0, c + per_weight) * inv[:, 0:1]
                 at = pl.ds(pl.multiple_of(c * width, width), width)
                 values[:, at] = value.astype(jnp.bfloat16)
+                result_copy(values, values_out, c, 3 + per_weight + c).start()
+
+    for copy in stores:
+        copy.wait()
+
+    @pl.loop(0, per_weight)
+    def _(c):
+        result_copy(keys, keys_out, c, 3 + c).wait()
+        result_copy(values, values_out, c, 3 + per_weight + c).wait()
 
     for copy in list(a_copies.values()) + b_copies + d_copies + o_copies:
         copy.wait_send()
@@ -289,9 +330,20 @@
             jax.ShapeDtypeStruct(own, jnp.float32),
             jax.ShapeDtypeStruct(local_params.shape[1:], jnp.bfloat16),
         ),
-        in_specs=[hbm, vmem, hbm, hbm] + [vmem] * 6,
-        out_specs=[vmem] * 5,
+        in_specs=[hbm, vmem] + [hbm] * 8,
+        out_specs=[hbm] * 5,
         scratch_shapes=[
+            pltpu.VMEM(cosine.shape, jnp.float32),
+            pltpu.VMEM(sine.shape, jnp.float32),
+            pltpu.VMEM(own, jnp.float32),
+            pltpu.VMEM(own, jnp.float32),
+            pltpu.VMEM(own, jnp.float32),
+            pltpu.VMEM(local_params.shape[1:], jnp.bfloat16),
+            pltpu.VMEM((tokens, kv), jnp.bfloat16),
+            pltpu.VMEM((tokens, kv), jnp.bfloat16),
+            pltpu.VMEM(own, jnp.float32),
+            pltpu.VMEM(own, jnp.float32),
+            pltpu.VMEM(local_params.shape[1:], jnp.bfloat16),
             pltpu.VMEM((tokens, features), jnp.bfloat16),
             pltpu.VMEM((2, 1, depth), jnp.bfloat16),
             pltpu.VMEM((groups - 1, tokens, 2 * depth), jnp.bfloat16),
@@ -311,6 +363,8 @@
             dma((2, len(plan), chunks)),
             dma((2, replicas - 1)),
             dma((2, replicas - 1)),
+            dma((6,)),
+            dma((3 + chunks,)),
         ],
         compiler_params=pltpu.CompilerParams(
             collective_id=0, has_side_effects=True, vmem_limit_bytes=60 * 1024 * 1024
@@ -322,10 +376,10 @@
     keys, values, momentum_new, outer_new, local_new = pl.pallas_call(
         write_out,
         out_shape=tuple(jax.ShapeDtypeStruct(a.shape, a.dtype) for a in results),
-        in_specs=[hbm] * 5,
+        in_specs=[vmem] * 5,
         out_specs=[hbm] * 5,
         scratch_shapes=[dma((5,))],
-        compiler_params=pltpu.CompilerParams(vmem_limit_bytes=1024 * 1024),
+        compiler_params=pltpu.CompilerParams(vmem_limit_bytes=60 * 1024 * 1024),
     )(*results)
     return keys[None], values[None], momentum_new, outer_new, local_new[None]
 

time: 124 us -> 120 us (0.968)
  local copies, waits for them, and re-layouts: 4.83 us -> 0 us
    unnamed x10 -> x0, local copies, waits for them, and re-layouts: 4.83 us -> none
    pallas_call x1, Pallas kernels: 1.17 us -> 2.52 us  [per_device(): pl.pallas_call(write_out, out_shape=tuple((jax.ShapeDtypeStruct(a.shape,...]
where the time goes in v3:
time: 120 us; the launch traced here: 119 us
  Pallas kernels  119 us (99%)
    pallas_call x1, Pallas kernels, per_device(): pl.pallas_call(functools.partial(kernel, groups, replicas, width), out_sh...  116 us
    pallas_call x1, Pallas kernels, per_device(): pl.pallas_call(write_out, out_shape=tuple((jax.ShapeDtypeStruct(a.shape,...  2.52 us

profile of v3, /device:TPU:0, one launch (start us, length us, event | category | flops | bytes accessed | tf_op | source)
XLA Modules:
  0.0 119.4 jit_solution(10439941003559844050)
XLA Ops:
  0.6 116.2 %shard_map.137 = (bf16[256,1024]{1,0:T(8,128)(2,1)}, bf16[256,1024]{1,0:T(8,128)(2,1)}, f32[32,1024]{1,0:T(8,128)}, f32[32,1024]{1,0:T(8,128)}, bf16[32,4096]{1,0:T(8,128)(2,1)}) custom-call(bf16[256,4096]{1,0:T(8,128)(2,1)} %bitcast.8, bf16[1,512]{1,0:T(2,128)(2,1)} %gain.1, bf16[512,1024]{1,0:T(8,128)(2,1)} %bitcast.9, bf16[512,1024]{1,0:T(8,128)(2,1)} %bitcast.10, ...), custom_call_target="tpu_custom_call" | custom-call | tf_op jit(solution)/shard_map/pallas_call | solution.py:324
  116.9 2.5 %shard_map.138 = (bf16[256,1024]{1,0:T(8,128)(2,1)}, bf16[256,1024]{1,0:T(8,128)(2,1)}, f32[32,1024]{1,0:T(8,128)}, f32[32,1024]{1,0:T(8,128)}, bf16[32,4096]{1,0:T(8,128)(2,1)}) custom-call(bf16[256,1024]{1,0:T(8,128)(2,1)} %get-tuple-element.15.refs_0_, bf16[256,1024]{1,0:T(8,128)(2,1)} %get-tuple-element.16.refs_1_, ...), custom_call_target="tpu_custom_call" | custom-call | tf_op jit(solution)/shard_map/pallas_call | solution.py:376

commit v4 on v3

--- a/solution.py
+++ b/solution.py
@@ -132,7 +132,7 @@
             a_copies[b] = remote(hs.at[:, columns], a_in.at[b - 1], a_sem, (b - 1,), peer(b))
             a_copies[b].start()
 
-    send_tokens(plan[0][1])
+    send_tokens(plan[0][1][::-1] + [b for b in plan[0][2] if b])
     b_copies = []
     for c in range(chunks):
         source = (kw if c < per_weight else vw).at[:, pl.ds((c % per_weight) * width, width)]
@@ -202,9 +202,7 @@
             c_out[0][c, i] = product(b, c).astype(jnp.bfloat16)
         c_copy(0, c).start()
 
-    pl.loop(0, 1)(first_products)
-    send_tokens([b for b in plan[0][2] if b])
-    pl.loop(1, chunks)(first_products)
+    pl.loop(0, chunks)(first_products)
 
     for copy in loads:
         copy.wait()

time: 120 us -> 117 us (0.975)
  Pallas kernels: 119 us -> 115 us
    pallas_call x1, Pallas kernels: 116 us -> 113 us  [per_device(): pl.pallas_call(functools.partial(kernel, groups, replicas, width), out_sh...]
where the time goes in v4:
time: 117 us; the launch traced here: 116 us
  Pallas kernels  115 us (98%)
    pallas_call x1, Pallas kernels, per_device(): pl.pallas_call(functools.partial(kernel, groups, replicas, width), out_sh...  113 us
    pallas_call x1, Pallas kernels, per_device(): pl.pallas_call(write_out, out_shape=tuple((jax.ShapeDtypeStruct(a.shape,...  2.52 us

profile of v4, /device:TPU:0, one launch (start us, length us, event | category | flops | bytes accessed | tf_op | source)
XLA Modules:
  0.0 116.0 jit_solution(15038454619035232749)
XLA Ops:
  0.6 112.9 %shard_map.137 = (bf16[256,1024]{1,0:T(8,128)(2,1)}, bf16[256,1024]{1,0:T(8,128)(2,1)}, f32[32,1024]{1,0:T(8,128)}, f32[32,1024]{1,0:T(8,128)}, bf16[32,4096]{1,0:T(8,128)(2,1)}) custom-call(bf16[256,4096]{1,0:T(8,128)(2,1)} %bitcast.8, bf16[1,512]{1,0:T(2,128)(2,1)} %gain.1, bf16[512,1024]{1,0:T(8,128)(2,1)} %bitcast.9, bf16[512,1024]{1,0:T(8,128)(2,1)} %bitcast.10, ...), custom_call_target="tpu_custom_call" | custom-call | tf_op jit(solution)/shard_map/pallas_call | solution.py:322
  113.5 2.5 %shard_map.138 = (bf16[256,1024]{1,0:T(8,128)(2,1)}, bf16[256,1024]{1,0:T(8,128)(2,1)}, f32[32,1024]{1,0:T(8,128)}, f32[32,1024]{1,0:T(8,128)}, bf16[32,4096]{1,0:T(8,128)(2,1)}) custom-call(bf16[256,1024]{1,0:T(8,128)(2,1)} %get-tuple-element.15.refs_0_, bf16[256,1024]{1,0:T(8,128)(2,1)} %get-tuple-element.16.refs_1_, ...), custom_call_target="tpu_custom_call" | custom-call | tf_op jit(solution)/shard_map/pallas_call | solution.py:374
